TPU v7x, 32 devices: a whole 2x2x4 slice. The times are simulated.
32 devices in a mesh: replica: 8 (over z, y), model: 4 (over x, core).
Axes of the slice: x: 2, y: 2, z: 4, core: 2. Of those that a mesh axis runs over, the one named last changes fastest.
Arguments:
- slope_query: bfloat16 [8, 1024, 1024], P('replica', None, 'model'), may hold values from -4 to 4
- slope_key: bfloat16 [8, 1024, 1024], P('replica', None, 'model'), may hold values from -4 to 4
- slope_value: bfloat16 [8, 1024, 1024], P('replica', None, 'model'), may hold values from -4 to 4
- slope_mixed: bfloat16 [8, 1024, 1024], P('replica', 'model'), may hold values from -4 to 4
- slope_norm: bfloat16 [8, 1024], P('replica'), may hold values from -8 to 8
- param_query: float32 [1024, 1024], P('replica', 'model'), may hold values from -0.25 to 0.25
- param_key: float32 [1024, 1024], P('replica', 'model'), may hold values from -0.25 to 0.25
- param_value: float32 [1024, 1024], P('replica', 'model'), may hold values from -0.25 to 0.25
- param_mixed: float32 [1024, 1024], P('model', 'replica'), may hold values from -0.25 to 0.25
- param_norm: float32 [1024], P('replica'), may hold values from 0.25 to 1.75
- state_query: float32 [1024, 1024], P('replica', 'model'), may hold values from 0.0001953125 to 0.001953125
- state_key: float32 [1024, 1024], P('replica', 'model'), may hold values from 0.0001953125 to 0.001953125
- state_value: float32 [1024, 1024], P('replica', 'model'), may hold values from 0.0001953125 to 0.001953125
- state_mixed: float32 [1024, 1024], P('model', 'replica'), may hold values from 0.0001953125 to 0.001953125
- state_norm: float32 [1024], P('replica'), may hold values from 0.05 to 0.8
Outputs:
- half_query: bfloat16 [1024, 1024], P(None, 'model')
- half_key: bfloat16 [1024, 1024], P(None, 'model')
- half_value: bfloat16 [1024, 1024], P(None, 'model')
- half_mixed: bfloat16 [1024, 1024], P('model')
- half_norm: bfloat16 [1024], replicated
- next_query: float32 [1024, 1024], P('replica', 'model')
- next_key: float32 [1024, 1024], P('replica', 'model')
- next_value: float32 [1024, 1024], P('replica', 'model')
- next_mixed: float32 [1024, 1024], P('model', 'replica')
- next_norm: float32 [1024], P('replica')
- state_new_query: float32 [1024, 1024], P('replica', 'model')
- state_new_key: float32 [1024, 1024], P('replica', 'model')
- state_new_value: float32 [1024, 1024], P('replica', 'model')
- state_new_mixed: float32 [1024, 1024], P('model', 'replica')
- state_new_norm: float32 [1024], P('replica')
All inputs are finite; a program needn't handle non-finite values.
Results may differ from a plain program's by a relative error of at most 0.001.
Values may be sent and summed in bfloat16 or wider, within the bound.
A program may use at most 64 MiB of HBM per device.

v0:
```python
import jax
import jax.numpy as jnp
from jax import lax
from jax.sharding import PartitionSpec as P

learn_rate = 0.025
hold_rate = 0.7


def local(
    slope_query,
    slope_key,
    slope_value,
    slope_mixed,
    slope_norm,
    param_query,
    param_key,
    param_value,
    param_mixed,
    param_norm,
    state_query,
    state_key,
    state_value,
    state_mixed,
    state_norm,
):
    mean_query, mean_key, mean_value, mean_mixed = (
        lax.psum_scatter(
            slope_query[0].astype(jnp.float32), "replica", scatter_dimension=0, tiled=True
        ),
        lax.psum_scatter(
            slope_key[0].astype(jnp.float32), "replica", scatter_dimension=0, tiled=True
        ),
        lax.psum_scatter(
            slope_value[0].astype(jnp.float32), "replica", scatter_dimension=0, tiled=True
        ),
        lax.psum_scatter(
            slope_mixed[0].astype(jnp.float32), "replica", scatter_dimension=1, tiled=True
        ),
    )
    whole_norm = lax.psum(slope_norm[0].astype(jnp.float32), "replica")
    place = lax.axis_index("replica")
    mean_norm = lax.dynamic_slice_in_dim(
        whole_norm, place * param_norm.shape[0], param_norm.shape[0]
    )
    mean_rate = lax.axis_size("replica") ** (-0.5)
    mean_query = mean_query * mean_rate
    mean_key = mean_key * mean_rate
    mean_value = mean_value * mean_rate
    mean_mixed = mean_mixed * mean_rate
    mean_norm = mean_norm * mean_rate
    (
        own_query,
        own_key,
        own_value,
        own_mixed,
        slope_query_norm,
        slope_key_norm,
        slope_value_norm,
        slope_mixed_norm,
    ) = lax.psum(
        (
            jnp.sum(param_query * param_query, axis=1, keepdims=True),
            jnp.sum(param_key * param_key, axis=1, keepdims=True),
            jnp.sum(param_value * param_value, axis=1, keepdims=True),
            jnp.sum(param_mixed * param_mixed, axis=0, keepdims=True),
            jnp.sum(mean_query * mean_query, axis=1, keepdims=True),
            jnp.sum(mean_key * mean_key, axis=1, keepdims=True),
            jnp.sum(mean_value * mean_value, axis=1, keepdims=True),
            jnp.sum(mean_mixed * mean_mixed, axis=0, keepdims=True),
        ),
        "model",
    )
    mean_query = mean_query * (jnp.sqrt(own_query) * lax.rsqrt(slope_query_norm + 1e-06))
    mean_key = mean_key * (jnp.sqrt(own_key) * lax.rsqrt(slope_key_norm + 1e-06))
    mean_value = mean_value * (jnp.sqrt(own_value) * lax.rsqrt(slope_value_norm + 1e-06))
    mean_mixed = mean_mixed * (jnp.sqrt(own_mixed) * lax.rsqrt(slope_mixed_norm + 1e-06))
    state_new_query = hold_rate * state_query + (1.0 - hold_rate) * mean_query * mean_query
    next_query = param_query - learn_rate * mean_query * lax.rsqrt(state_new_query + 1e-06)
    state_new_key = hold_rate * state_key + (1.0 - hold_rate) * mean_key * mean_key
    next_key = param_key - learn_rate * mean_key * lax.rsqrt(state_new_key + 1e-06)
    state_new_value = hold_rate * state_value + (1.0 - hold_rate) * mean_value * mean_value
    next_value = param_value - learn_rate * mean_value * lax.rsqrt(state_new_value + 1e-06)
    state_new_mixed = hold_rate * state_mixed + (1.0 - hold_rate) * mean_mixed * mean_mixed
    next_mixed = param_mixed - learn_rate * mean_mixed * lax.rsqrt(state_new_mixed + 1e-06)
    state_new_norm = hold_rate * state_norm + (1.0 - hold_rate) * mean_norm * mean_norm
    next_norm = param_norm - learn_rate * mean_norm * lax.rsqrt(state_new_norm + 1e-06)
    half_query, half_key, half_value, half_mixed, half_norm = (
        lax.all_gather(next_query.astype(jnp.bfloat16), "replica", axis=0, tiled=True),
        lax.all_gather(next_key.astype(jnp.bfloat16), "replica", axis=0, tiled=True),
        lax.all_gather(next_value.astype(jnp.bfloat16), "replica", axis=0, tiled=True),
        lax.all_gather(next_mixed.astype(jnp.bfloat16), "replica", axis=1, tiled=True),
        lax.all_gather(next_norm.astype(jnp.bfloat16), "replica", axis=0, tiled=True),
    )
    return (
        half_query,
        half_key,
        half_value,
        half_mixed,
        half_norm,
        next_query,
        next_key,
        next_value,
        next_mixed,
        next_norm,
        state_new_query,
        state_new_key,
        state_new_value,
        state_new_mixed,
        state_new_norm,
    )


def solution(mesh):
    return jax.shard_map(
        local,
        mesh=mesh,
        in_specs=(
            P("replica", None, "model"),
            P("replica", None, "model"),
            P("replica", None, "model"),
            P("replica", "model", None),
            P("replica", None),
            P("replica", "model"),
            P("replica", "model"),
            P("replica", "model"),
            P("model", "replica"),
            P("replica"),
            P("replica", "model"),
            P("replica", "model"),
            P("replica", "model"),
            P("model", "replica"),
            P("replica"),
        ),
        out_specs=(
            P(None, "model"),
            P(None, "model"),
            P(None, "model"),
            P("model", None),
            P(),
            P("replica", "model"),
            P("replica", "model"),
            P("replica", "model"),
            P("model", "replica"),
            P("replica"),
            P("replica", "model"),
            P("replica", "model"),
            P("replica", "model"),
            P("model", "replica"),
            P("replica"),
        ),
        check_vma=False,
    )
```

profile of v0, /device:TPU:0, one launch (start us, length us, event | category | flops | bytes accessed | tf_op | source)
XLA Modules:
  0.0 420.6 jit_solution(1416145963046839783)
XLA Ops:
  7.2 0.0 reduce-scatter.9.cloned.1.call-start
  7.2 2.1 bitcast_convert_fusion.1
  9.3 0.0 copy-start
  9.3 0.0 reduce-scatter.9.cloned.1.call-update
  9.4 0.0 reduce-scatter.11.cloned.1.call-start
  9.4 1.0 copy-done
  10.4 1.1 bitcast_convert_fusion
  11.5 0.0 copy-start.1
  11.5 0.0 reduce-scatter.11.cloned.1.call-update
  11.6 0.0 reduce-scatter.5.cloned.1.call-start
  11.6 1.0 copy-done.1
  12.6 1.1 bitcast_convert_fusion.3
  13.6 0.0 copy-start.2
  13.6 0.0 reduce-scatter.5.cloned.1.call-update
  13.7 0.0 reduce-scatter.7.cloned.1.call-start
  13.7 1.0 copy-done.2
  14.7 1.1 bitcast_convert_fusion.2
  15.7 0.0 reduce-scatter.7.cloned.1.call-update
  15.8 0.0 copy-start.5
  15.8 0.6 copy-done.15
  16.4 23.2 %psum.71 = f32[1024]{0:T(1024)S(1)} all-reduce(f32[1024]{0:T(1024)S(1)} %bitcast.32), channel_id=1, replica_groups=mesh['replica'=8,'model'=4] {'replica'}, use_global_device_ids=true, to_apply=%region_20.0 | all-reduce | flops 1024 | bytes 8192 | tf_op jit(solution)/shard_map/psum | solution.py:41
  39.6 0.0 copy-done.16
  39.6 0.0 copy-done.17
  39.6 0.6 convert_bitcast_fusion
  40.2 16.3 %all-gather = bf16[8,1,128]{2,1,0:T(2,128)(2,1)S(1)} all-gather(bf16[1,1,128]{2,1,0:T(2,128)(2,1)S(1)} %get-tuple-element.23), channel_id=1, replica_groups=mesh['replica'=8,'model'=4] {'replica'}, dimensions={0}, use_global_device_ids=true | all-gather | bytes 2304 | tf_op jit(solution)/shard_map/all_gather | solution.py:93
  56.5 0.6 reduce
  57.1 0.0 copy-done.6
  57.1 0.1 multiply_reduce_fusion.7
  57.2 0.0 copy-done.5
  57.2 0.0 copy-start.3
  57.3 0.7 copy-done.4
  58.0 0.1 multiply_reduce_fusion.5
  58.1 0.0 copy-done.3
  58.1 0.1 multiply_reduce_fusion.3
  58.3 20.4 %reduce-scatter.9.cloned.1.call-done = f32[128,256]{1,0:T(8,128)} async-done(((f32[1024,256]{1,0:T(8,128)}), f32[128,256]{1,0:T(8,128)}) %reduce-scatter.9.cloned.1.call-update) | async-done | bytes 131088 | tf_op jit(solution)/shard_map/reduce_scatter | solution.py:34
  78.7 1.0 multiply_reduce_fusion.2
  79.7 66.0 %reduce-scatter.11.cloned.1.call-done = f32[256,128]{1,0:T(8,128)} async-done(((f32[256,1024]{1,0:T(8,128)}), f32[256,128]{1,0:T(8,128)}) %reduce-scatter.11.cloned.1.call-update) | async-done | bytes 131088 | tf_op jit(solution)/shard_map/reduce_scatter | solution.py:37
  145.7 1.0 multiply_reduce_fusion
  146.7 0.0 copy-start.11
  146.7 65.7 %reduce-scatter.5.cloned.1.call-done = f32[128,256]{1,0:T(8,128)} async-done(((f32[1024,256]{1,0:T(8,128)}), f32[128,256]{1,0:T(8,128)}) %reduce-scatter.5.cloned.1.call-update) | async-done | bytes 131088 | tf_op jit(solution)/shard_map/reduce_scatter | solution.py:28
  212.4 1.0 multiply_reduce_fusion.6
  213.4 65.5 %reduce-scatter.7.cloned.1.call-done = f32[128,256]{1,0:T(8,128)} async-done(((f32[1024,256]{1,0:T(8,128)}), f32[128,256]{1,0:T(8,128)}) %reduce-scatter.7.cloned.1.call-update) | async-done | bytes 131088 | tf_op jit(solution)/shard_map/reduce_scatter | solution.py:31
  278.9 1.0 multiply_reduce_fusion.4
  279.9 5.7 %all-reduce = (f32[128,1]{0,1:T(1,128)S(1)}, f32[128,1]{0,1:T(1,128)S(1)}, f32[128,1]{0,1:T(1,128)S(1)}, f32[128,1]{0,1:T(1,128)S(1)}, f32[128,1]{0,1:T(1,128)S(...) all-reduce(f32[128,1]{0,1:T(1,128)S(1)} %bitcast.39, ...), channel_id=1, replica_groups=mesh['replica'=8,'model'=4] {'model'}, use_global_device_ids=true, to_apply=%region_4.0 | all-reduce | flops 1024 | bytes 8192 | tf_op jit(solution)/shard_map/psum | solution.py:61
  285.6 0.0 copy-done.9
  285.6 0.0 copy-done.11
  285.6 0.8 fusion.6
  286.4 31.6 %all_gather.17 = bf16[1024,256]{1,0:T(8,128)(2,1)S(1)} all-gather(bf16[128,256]{1,0:T(8,128)(2,1)S(1)} %get-tuple-element.29), channel_id=1, replica_groups=mesh['replica'=8,'model'=4] {'replica'}, dimensions={0}, use_global_device_ids=true | all-gather | bytes 589824 | tf_op jit(solution)/shard_map/all_gather | solution.py:91
  318.0 0.0 copy-done.10
  318.0 0.0 copy-done.12
  318.0 0.8 fusion.8
  318.8 31.5 %all_gather.16 = bf16[1024,256]{1,0:T(8,128)(2,1)S(1)} all-gather(bf16[128,256]{1,0:T(8,128)(2,1)S(1)} %get-tuple-element.32), channel_id=1, replica_groups=mesh['replica'=8,'model'=4] {'replica'}, dimensions={0}, use_global_device_ids=true | all-gather | bytes 589824 | tf_op jit(solution)/shard_map/all_gather | solution.py:90
  350.3 0.0 copy-done.8
  350.3 0.0 copy-done.13
  350.3 0.7 fusion.4
  351.0 27.9 %all_gather.18 = bf16[256,1024]{1,0:T(8,128)(2,1)S(1)} all-gather(bf16[256,128]{1,0:T(8,128)(2,1)S(1)} %get-tuple-element.26), channel_id=1, replica_groups=mesh['replica'=8,'model'=4] {'replica'}, dimensions={1}, use_global_device_ids=true | all-gather | bytes 589824 | tf_op jit(solution)/shard_map/all_gather | solution.py:92
  378.9 0.0 copy-done.7
  378.9 0.0 copy-done.14
  379.0 0.8 fusion.10
  379.8 31.2 %all_gather.15 = bf16[1024,256]{1,0:T(8,128)(2,1)S(1)} all-gather(bf16[128,256]{1,0:T(8,128)(2,1)S(1)} %get-tuple-element.35), channel_id=1, replica_groups=mesh['replica'=8,'model'=4] {'replica'}, dimensions={0}, use_global_device_ids=true | all-gather | bytes 589824 | tf_op jit(solution)/shard_map/all_gather | solution.py:89
  410.9 0.8 copy.34
  411.7 0.8 copy.35
  412.5 0.8 copy.36
  413.3 0.8 copy.37
  (17 shorter events, 0.1 us)
Async XLA Ops:
  7.2 71.5 %reduce-scatter.9.cloned.1.call-start = ((), (), s32[]{:S(2)}) async-start(), calls=%async_computation.6 | async-start | bytes 1179648 | tf_op jit(solution)/shard_map/reduce_scatter | solution.py:34
  9.3 1.0 copy-start
  9.4 136.4 %reduce-scatter.11.cloned.1.call-start = ((), (), s32[]{:S(2)}) async-start(), calls=%async_computation.7 | async-start | bytes 1179648 | tf_op jit(solution)/shard_map/reduce_scatter | solution.py:37
  11.5 1.0 copy-start.1
  11.6 200.8 %reduce-scatter.5.cloned.1.call-start = ((), (), s32[]{:S(2)}) async-start(), calls=%async_computation.4 | async-start | bytes 1179648 | tf_op jit(solution)/shard_map/reduce_scatter | solution.py:28
  13.6 1.0 copy-start.2
  13.7 265.2 %reduce-scatter.7.cloned.1.call-start = ((), (), s32[]{:S(2)}) async-start(), calls=%async_computation.5 | async-start | bytes 1179648 | tf_op jit(solution)/shard_map/reduce_scatter | solution.py:31
  15.7 0.7 copy-start.15
  15.7 23.9 %copy-start.16 = (f32[128]{0:T(128)S(1)}, f32[128]{0:T(128)}, u32[]{:S(2)}) copy-start(f32[128]{0:T(128)} %param.24) | copy-start | bytes 1540
  15.7 23.9 %copy-start.17 = (f32[128]{0:T(128)S(1)}, f32[128]{0:T(128)}, u32[]{:S(2)}) copy-start(f32[128]{0:T(128)} %param.29) | copy-start | bytes 1540
  15.7 41.4 %copy-start.6 = (f32[128,256]{1,0:T(8,128)S(1)}, f32[128,256]{1,0:T(8,128)}, u32[]{:S(2)}) copy-start(f32[128,256]{1,0:T(8,128)} %param.20) | copy-start | bytes 393220
  15.8 41.5 %copy-start.5 = (f32[256,128]{1,0:T(8,128)S(1)}, f32[256,128]{1,0:T(8,128)}, u32[]{:S(2)}) copy-start(f32[256,128]{1,0:T(8,128)} %param.23) | copy-start | bytes 393220
  57.1 0.9 copy-start.4
  57.2 0.9 copy-start.3
  146.7 138.9 %copy-start.9 = (f32[128,256]{1,0:T(8,128)S(1)}, f32[128,256]{1,0:T(8,128)}, u32[]{:S(2)}) copy-start(f32[128,256]{1,0:T(8,128)} %reduce-scatter.9.cloned.1.call-done) | copy-start | bytes 393220
  146.7 138.9 %copy-start.11 = (f32[128,256]{1,0:T(8,128)S(1)}, f32[128,256]{1,0:T(8,128)}, u32[]{:S(2)}) copy-start(f32[128,256]{1,0:T(8,128)} %param.27) | copy-start | bytes 393220
  286.4 31.6 %copy-start.10 = (f32[128,256]{1,0:T(8,128)S(1)}, f32[128,256]{1,0:T(8,128)}, u32[]{:S(2)}) copy-start(f32[128,256]{1,0:T(8,128)} %reduce-scatter.7.cloned.1.call-done) | copy-start | bytes 393220
  286.4 31.6 %copy-start.12 = (f32[128,256]{1,0:T(8,128)S(1)}, f32[128,256]{1,0:T(8,128)}, u32[]{:S(2)}) copy-start(f32[128,256]{1,0:T(8,128)} %param.26) | copy-start | bytes 393220
  318.8 31.5 %copy-start.8 = (f32[256,128]{1,0:T(8,128)S(1)}, f32[256,128]{1,0:T(8,128)}, u32[]{:S(2)}) copy-start(f32[256,128]{1,0:T(8,128)} %reduce-scatter.11.cloned.1.call-done) | copy-start | bytes 393220
  318.8 31.5 %copy-start.13 = (f32[256,128]{1,0:T(8,128)S(1)}, f32[256,128]{1,0:T(8,128)}, u32[]{:S(2)}) copy-start(f32[256,128]{1,0:T(8,128)} %param.28) | copy-start | bytes 393220
  351.0 27.9 %copy-start.7 = (f32[128,256]{1,0:T(8,128)S(1)}, f32[128,256]{1,0:T(8,128)}, u32[]{:S(2)}) copy-start(f32[128,256]{1,0:T(8,128)} %reduce-scatter.5.cloned.1.call-done) | copy-start | bytes 393220
  351.0 27.9 %copy-start.14 = (f32[128,256]{1,0:T(8,128)S(1)}, f32[128,256]{1,0:T(8,128)}, u32[]{:S(2)}) copy-start(f32[128,256]{1,0:T(8,128)} %param.25) | copy-start | bytes 393220
Sparse Core Ops, SparseCore 0:
  11.4 67.2 reduce-scatter.8
  82.1 63.5 reduce-scatter.10
  149.1 63.1 reduce-scatter.4
  215.6 63.1 reduce-scatter.6
where the time goes:
time: 421 us
  waiting for transfers between devices  218 us (52%)
  blocking collectives  167 us (40%)
  other arithmetic  14.1 us (3%)
  between operations  13.9 us (3%)
  local copies, waits for them, and re-layouts  7.52 us (2%)
    reduce_scatter x1, waiting for transfers between devices, local(): lax.psum_scatter(slope_mixed[0].astype(jnp.float32), 'replica', scatter_d...  66 us
    reduce_scatter x1, waiting for transfers between devices, local(): lax.psum_scatter(slope_query[0].astype(jnp.float32), 'replica', scatter_d...  65.7 us
    reduce_scatter x1, waiting for transfers between devices, local(): lax.psum_scatter(slope_key[0].astype(jnp.float32), 'replica', scatter_dim...  65.5 us
    all_gather x1, blocking collectives, local(): lax.all_gather(next_value.astype(jnp.bfloat16), 'replica', axis=0, tiled=...  31.6 us
    all_gather x1, blocking collectives, local(): lax.all_gather(next_key.astype(jnp.bfloat16), 'replica', axis=0, tiled=True)  31.5 us
    all_gather x1, blocking collectives, local(): lax.all_gather(next_query.astype(jnp.bfloat16), 'replica', axis=0, tiled=...  31.2 us
    all_gather x1, blocking collectives, local(): lax.all_gather(next_mixed.astype(jnp.bfloat16), 'replica', axis=1, tiled=...  27.9 us
    psum x1, blocking collectives, local(): whole_norm = lax.psum(slope_norm[0].astype(jnp.float32), 'replica')  23.2 us
  transfers between devices with their start and end apart: 4, of which 4 were waited for; matrix products, arithmetic and copies ran while one was open for 2% of the time, Pallas kernels for 0%

commit v1 on v0

v1 whole, which is shorter than its diff:
```python
import functools

import jax
import jax.numpy as jnp
from jax import lax
from jax.experimental import pallas as pl
from jax.experimental.pallas import tpu as pltpu
from jax.sharding import PartitionSpec as P

learn_rate = 0.025
hold_rate = 0.7
MESH = pl.DeviceIdType.MESH
LANES = 128
INNER = 2


def updated(param, mean, state):
    state_new = hold_rate * state + (1.0 - hold_rate) * mean * mean
    return param - learn_rate * mean * lax.rsqrt(state_new + 1e-06), state_new


def kernel(n, models, *refs):
    slopes, slope_norm = refs[0:4], refs[4]
    params, param_norm = refs[5:9], refs[9]
    states, state_norm = refs[10:14], refs[14]
    halves, half_norm = refs[15:19], refs[19]
    nexts, next_norm = refs[20:24], refs[24]
    state_news, state_new_norm = refs[25:29], refs[29]
    pair, ups, downs, totals = refs[30:34], refs[34:38], refs[38:42], refs[42:46]
    (
        own_sizes, mean_sizes, vector, parts,
        pair_send, pair_recv, up_send, up_recv, down_send, down_recv,
        give_up_send, give_up_recv, give_down_send, give_down_recv, give_pair_send, give_pair_recv,
        own_send, own_recv, mean_send, mean_recv,
        parts_send, parts_recv, norm_send, norm_recv,
    ) = refs[46:]
    outer = n // INNER
    rate = n ** (-0.5)
    me = lax.axis_index("replica")
    here = lax.axis_index("model")
    z, y = me // INNER, me % INNER
    width = param_norm.shape[1]
    partner = {"replica": z * INNER + (1 - y)}
    above = {"replica": lax.rem(me + INNER, n)}
    below = {"replica": lax.rem(me + n - INNER, n)}

    def block(m, ref, b):
        if m < 3:
            rows = params[m].shape[0]
            return ref.at[pl.ds(pl.multiple_of(b * rows, rows), rows), :]
        columns = params[m].shape[1]
        return ref.at[:, pl.ds(pl.multiple_of(b * columns, columns), columns)]

    def raw(m, b):
        return block(m, slopes[m].at[0], b)

    def remote(src, dst, send_sem, recv_sem, device):
        return pltpu.make_async_remote_copy(
            src_ref=src, dst_ref=dst, send_sem=send_sem, recv_sem=recv_sem,
            device_id=device, device_id_type=MESH,
        )

    def turn(i):
        return jnp.where(z < outer // 2, outer - 1 - i, i)

    def pair_copy(m, d):
        return remote(raw(m, d * INNER + (1 - y)), pair[m].at[d], pair_send.at[m, d], pair_recv.at[m, d], partner)

    def up_copy(m, d):
        return remote(ups[m].at[d], ups[m].at[d], up_send.at[m, d], up_recv.at[m, d], above)

    def down_copy(m, d):
        return remote(downs[m].at[d], downs[m].at[d], down_send.at[m, d], down_recv.at[m, d], below)

    def give_up(m, s):
        place = block(m, halves[m], s * INNER + y)
        return remote(place, place, give_up_send.at[m, s], give_up_recv.at[m, s], above)

    def give_down(m, s):
        place = block(m, halves[m], s * INNER + y)
        return remote(place, place, give_down_send.at[m, s], give_down_recv.at[m, s], below)

    def give_pair(m, s, side):
        place = block(m, halves[m], s * INNER + side)
        return remote(place, place, give_pair_send.at[m, s], give_pair_recv.at[m, s], partner)

    def own_copy(k):
        peer = lax.rem(here + k, models)
        return peer, remote(own_sizes.at[here], own_sizes.at[here], own_send.at[k], own_recv.at[here], {"model": peer})

    def mean_copy(m, k):
        peer = lax.rem(here + k, models)
        place = mean_sizes.at[m, here]
        return peer, remote(place, place, mean_send.at[m, k], mean_recv.at[m, here], {"model": peer})

    def parts_copy(k):
        peer = lax.rem(me + k, n)
        src = vector.at[:, pl.ds(pl.multiple_of(peer * width, width), width)]
        return peer, remote(src, parts.at[me], parts_send.at[k], parts_recv.at[me], {"replica": peer})

    def norm_copy(k):
        peer = lax.rem(me + k, n)
        return peer, remote(half_norm.at[me], half_norm.at[me], norm_send.at[k], norm_recv.at[me], {"replica": peer})

    def local_sum(m, d):
        return raw(m, d * INNER + y)[...].astype(jnp.float32) + pair[m][d].astype(jnp.float32)

    def sizes(m, value):
        square = value * value
        if m < 3:
            rows = square.shape[0]
            column = jnp.sum(square, axis=1, keepdims=True)
            return jnp.broadcast_to(column, (rows, LANES)).T[0:8]
        return jnp.broadcast_to(jnp.sum(square, axis=0, keepdims=True), (8, square.shape[1]))

    def send_sums(m):
        for i in range(outer):
            d = turn(i)
            pair_copy(m, d).wait_recv()

            @pl.when(d > z)
            def _():
                @pl.when(z > 0)
                def _():
                    up_copy(m, d).wait_recv()
                    ups[m][d] = ups[m][d] + local_sum(m, d)

                @pl.when(z == 0)
                def _():
                    ups[m][d] = local_sum(m, d)

                up_copy(m, d).start()

            @pl.when(d < z)
            def _():
                @pl.when(z < outer - 1)
                def _():
                    down_copy(m, d).wait_recv()
                    downs[m][d] = downs[m][d] + local_sum(m, d)

                @pl.when(z == outer - 1)
                def _():
                    downs[m][d] = local_sum(m, d)

                down_copy(m, d).start()

    def finish_sum(m):
        totals[m][...] = local_sum(m, z)

        @pl.when(z > 0)
        def _():
            up_copy(m, z).wait_recv()
            totals[m][...] += ups[m][z]

        @pl.when(z < outer - 1)
        def _():
            down_copy(m, z).wait_recv()
            totals[m][...] += downs[m][z]

        mean = totals[m][...] * rate
        totals[m][...] = mean
        mean_sizes[m, here] = sizes(m, mean)
        for k in range(1, models):
            mean_copy(m, k)[1].start()

    def update(m):
        for k in range(1, models):
            peer = lax.rem(here + k, models)
            place = mean_sizes.at[m, peer]
            remote(place, place, mean_send.at[m, k], mean_recv.at[m, peer], {"model": peer}).wait_recv()
        own = own_sizes[0, m]
        size = mean_sizes[m, 0]
        for k in range(1, models):
            own = own + own_sizes[k, m]
            size = size + mean_sizes[m, k]
        ratio = (jnp.sqrt(own) * lax.rsqrt(size + 1e-06))[0:1]
        shape = params[m].shape
        if m < 3:
            tile = jnp.broadcast_to(ratio, (LANES, shape[0])).T
            ratio = jnp.concatenate([tile] * (shape[1] // LANES), axis=1)
        next_value, state_new = updated(params[m][...], totals[m][...] * ratio, states[m][...])
        nexts[m][...] = next_value
        state_news[m][...] = state_new
        block(m, halves[m], me)[...] = next_value.astype(jnp.bfloat16)

        @pl.when(z < outer - 1)
        def _():
            give_up(m, z).start()

        @pl.when(z > 0)
        def _():
            give_down(m, z).start()

        give_pair(m, z, y).start()

    def relay(m):
        for k in range(1, outer):
            @pl.when(z >= k)
            def _():
                s = z - k
                give_up(m, s).wait_recv()

                @pl.when(z < outer - 1)
                def _():
                    give_up(m, s).start()

                give_pair(m, s, y).start()

            @pl.when(z + k < outer)
            def _():
                s = z + k
                give_down(m, s).wait_recv()

                @pl.when(z > 0)
                def _():
                    give_down(m, s).start()

                give_pair(m, s, y).start()

    def close(m):
        for s in range(outer):
            give_pair(m, s, 1 - y).wait_recv()
        for s in range(outer):
            pair_copy(m, s).wait_send()
            give_pair(m, s, y).wait_send()

            @pl.when(s > z)
            def _():
                up_copy(m, s).wait_send()

            @pl.when(s < z)
            def _():
                down_copy(m, s).wait_send()

            @pl.when(jnp.logical_and(s <= z, z < outer - 1))
            def _():
                give_up(m, s).wait_send()

            @pl.when(jnp.logical_and(s >= z, z > 0))
            def _():
                give_down(m, s).wait_send()

        for k in range(1, models):
            mean_copy(m, k)[1].wait_send()

    def vector_update():
        for k in range(1, n):
            peer = lax.rem(me + k, n)
            remote(parts.at[peer], parts.at[peer], parts_send.at[k], parts_recv.at[peer], {"replica": peer}).wait_recv()
        mean = parts[0]
        for k in range(1, n):
            mean = mean + parts[k]
        next_value, state_new = updated(param_norm[...], mean * rate, state_norm[...])
        next_norm[...] = next_value
        state_new_norm[...] = state_new
        half_norm[me] = next_value
        for k in range(1, n):
            norm_copy(k)[1].start()

    barrier = pltpu.get_barrier_semaphore()
    for k in range(1, n):
        pl.semaphore_signal(barrier, inc=1, device_id={"replica": lax.rem(me + k, n)}, device_id_type=MESH)
    for k in range(1, models):
        pl.semaphore_signal(barrier, inc=1, device_id={"model": lax.rem(here + k, models)}, device_id_type=MESH)
    for m in range(4):
        own_sizes[here, m] = sizes(m, params[m][...])
    vector[...] = slope_norm[...].astype(jnp.float32)
    parts[me] = vector[:, pl.ds(pl.multiple_of(me * width, width), width)]
    pl.semaphore_wait(barrier, n - 1 + models - 1)

    for m in range(4):
        for i in range(outer):
            pair_copy(m, turn(i)).start()
        if m == 0:
            for k in range(1, models):
                own_copy(k)[1].start()
            for k in range(1, n):
                parts_copy(k)[1].start()

    send_sums(0)
    vector_update()
    for k in range(1, models):
        peer = lax.rem(here + k, models)
        remote(own_sizes.at[peer], own_sizes.at[peer], own_send.at[k], own_recv.at[peer], {"model": peer}).wait_recv()
    send_sums(1)
    finish_sum(0)
    send_sums(2)
    update(0)
    finish_sum(1)
    send_sums(3)
    update(1)
    relay(0)
    finish_sum(2)
    update(2)
    relay(1)
    finish_sum(3)
    relay(2)
    update(3)
    relay(3)
    for m in range(4):
        close(m)
    for k in range(1, models):
        own_copy(k)[1].wait_send()
    for k in range(1, n):
        peer = lax.rem(me + k, n)
        remote(half_norm.at[peer], half_norm.at[peer], norm_send.at[k], norm_recv.at[peer], {"replica": peer}).wait_recv()
        parts_copy(k)[1].wait_send()
        norm_copy(k)[1].wait_send()


def fused(n, models, *args):
    slopes, params, states = args[0:5], args[5:10], args[10:15]
    outer = n // INNER
    width = params[4].shape[0]
    row = lambda a: a.reshape(1, width)
    shapes = [p.shape for p in params[0:4]]
    f32 = lambda s: jax.ShapeDtypeStruct(s, jnp.float32)
    out_shape = (
        [jax.ShapeDtypeStruct(s.shape[1:], jnp.bfloat16) for s in slopes[0:4]]
        + [f32((n, 1, width))]
        + ([f32(s) for s in shapes] + [f32((1, width))]) * 2
    )
    dma = lambda *s: pltpu.SemaphoreType.DMA(s)
    scratch = (
        [pltpu.VMEM((outer,) + s, jnp.bfloat16) for s in shapes]
        + [pltpu.VMEM((outer,) + s, jnp.float32) for s in shapes] * 2
        + [pltpu.VMEM(s, jnp.float32) for s in shapes]
        + [
            pltpu.VMEM((models, 4, 8, shapes[0][0]), jnp.float32),
            pltpu.VMEM((4, models, 8, shapes[0][0]), jnp.float32),
            pltpu.VMEM(slopes[4].shape, jnp.float32),
            pltpu.VMEM((n, 1, width), jnp.float32),
        ]
        + [dma(4, outer)] * 12
        + [dma(models)] * 2
        + [dma(4, models)] * 2
        + [dma(n)] * 4
    )
    outs = pl.pallas_call(
        functools.partial(kernel, n, models),
        out_shape=out_shape,
        in_specs=[pl.BlockSpec(memory_space=pltpu.VMEM)] * 15,
        out_specs=[pl.BlockSpec(memory_space=pltpu.VMEM)] * 15,
        scratch_shapes=scratch,
        compiler_params=pltpu.CompilerParams(collective_id=0, has_side_effects=True),
    )(*slopes, *params[0:4], row(params[4]), *states[0:4], row(states[4]))
    outs = list(outs)
    outs[4] = outs[4].reshape(-1).astype(jnp.bfloat16)
    outs[9] = outs[9].reshape(-1)
    outs[14] = outs[14].reshape(-1)
    return tuple(outs)


def plain(*args):
    slopes, params, states = args[0:5], args[5:10], args[10:15]
    rate = lax.axis_size("replica") ** (-0.5)
    dims = (0, 0, 0, 1)
    means = [
        lax.psum_scatter(s[0].astype(jnp.float32), "replica", scatter_dimension=d, tiled=True) * rate
        for s, d in zip(slopes, dims)
    ]
    whole = lax.psum(slopes[4][0].astype(jnp.float32), "replica")
    width = params[4].shape[0]
    mean_norm = lax.dynamic_slice_in_dim(whole, lax.axis_index("replica") * width, width) * rate
    size = lambda a, d: jnp.sum(a * a, axis=1 - d, keepdims=True)
    own, got = lax.psum(
        ([size(p, d) for p, d in zip(params, dims)], [size(a, d) for a, d in zip(means, dims)]), "model"
    )
    means = [a * (jnp.sqrt(o) * lax.rsqrt(g + 1e-06)) for a, o, g in zip(means, own, got)] + [mean_norm]
    pairs = [updated(p, a, s) for p, a, s in zip(params, means, states)]
    halves = [
        lax.all_gather(v.astype(jnp.bfloat16), "replica", axis=d, tiled=True)
        for (v, _), d in zip(pairs, dims + (0,))
    ]
    return tuple(halves) + tuple(v for v, _ in pairs) + tuple(s for _, s in pairs)


def solution(mesh):
    n, models = mesh.shape["replica"], mesh.shape["model"]

    def local(*args):
        rows, columns, width = args[5].shape[0], args[8].shape[1], args[9].shape[0]
        aligned = rows % LANES == 0 and columns % LANES == 0 and width % LANES == 0
        if n % INNER == 0 and aligned and rows == columns:
            return fused(n, models, *args)
        return plain(*args)

    inner, turned = P("replica", "model"), P("model", "replica")
    slices = (P("replica", None, "model"),) * 3 + (P("replica", "model", None), P("replica", None))
    shares = (inner,) * 3 + (turned, P("replica"))
    return jax.shard_map(
        local,
        mesh=mesh,
        in_specs=slices + shares * 2,
        out_specs=(P(None, "model"),) * 3 + (P("model", None), P()) + shares * 2,
        check_vma=False,
    )
```

time: 421 us -> 102 us (0.24)
  waiting for transfers between devices: 218 us -> 0 us
  blocking collectives: 167 us -> 0 us
  Pallas kernels: 0 us -> 86.5 us
  other arithmetic: 14.1 us -> 0.6 us
  between operations: 13.9 us -> 0.69 us
  local copies, waits for them, and re-layouts: 7.52 us -> 14.1 us
    reduce_scatter x4 -> x0, waiting for transfers between devices: 218 us -> none  [the longest x1 66 us: local(): lax.psum_scatter(slope_mixed[0].astype(jnp.float32), 'replica', scatter_d...]
    all_gather x5 -> x0, blocking collectives: 138 us -> none  [the longest x1 31.6 us: local(): lax.all_gather(next_value.astype(jnp.bfloat16), 'replica', axis=0, tiled=...]
    pallas_call x0 -> x1, Pallas kernels: none -> 86.5 us  [fused(): pl.pallas_call(functools.partial(kernel, n, models), out_shape=out_shape,...]
    psum x2 -> x0, blocking collectives: 28.9 us -> none  [the longest x1 23.2 us: local(): whole_norm = lax.psum(slope_norm[0].astype(jnp.float32), 'replica')]
    convert_element_type x9 -> x1, other arithmetic: 8.55 us -> 0.6 us  [fused(): outs[4] = outs[4].reshape(-1).astype(jnp.bfloat16)]
    unnamed x40 -> x42, local copies, waits for them, and re-layouts: 7.52 us -> 14.1 us
    reduce_sum x8 -> x0, other arithmetic: 4.33 us -> none  [the longest x1 1.01 us: local(): jnp.sum(mean_value * mean_value, axis=1, keepdims=True)]
  transfers between devices with their start and end apart: 4 -> 0, of which waited for: 4 -> 0; matrix products, arithmetic and copies ran while one was open for 2% -> 0% of each run, Pallas kernels for 0% -> 0%
where the time goes in v1:
time: 102 us
  Pallas kernels  86.5 us (85%)
  local copies, waits for them, and re-layouts  14.1 us (14%)
    pallas_call x1, Pallas kernels, fused(): pl.pallas_call(functools.partial(kernel, n, models), out_shape=out_shape,...  86.5 us
    unnamed x42, local copies, waits for them, and re-layouts  14.1 us

profile of v1, /device:TPU:0, one launch (start us, length us, event | category | flops | bytes accessed | tf_op | source)
XLA Modules:
  0.0 101.9 jit_solution(7415552185301714950)
XLA Ops:
  0.7 86.5 %shard_map.262 = (bf16[1024,256]{1,0:T(8,128)(2,1)}, bf16[1024,256]{1,0:T(8,128)(2,1)}, bf16[1024,256]{1,0:T(8,128)(2,1)}, bf16[256,1024]{1,0:T(8,128)(2,1)}, f3...) custom-call(bf16[1,1024,256]{2,1,0:T(8,128)(2,1)} %refs_0_.1, ...), custom_call_target="tpu_custom_call" | custom-call | tf_op jit(solution)/shard_map/pallas_call | solution.py:339
  87.1 0.0 copy-start.11
  87.1 0.7 copy-done.11
  87.8 0.6 convert_reduce_fusion
  88.4 0.0 copy-start.2
  88.4 1.9 %copy.44 = bf16[1024,256]{1,0:T(8,128)(2,1)} copy(bf16[1024,256]{1,0:T(8,128)(2,1)} %get-tuple-element.60) | data formatting | bytes 1048576
  90.3 0.0 copy-done.2
  90.3 0.0 copy-start.1
  90.4 0.8 copy.45
  91.1 0.4 copy-done.1
  91.6 0.0 copy-start
  91.6 0.8 copy.46
  92.4 0.4 copy-done
  92.8 0.0 copy-start.10
  92.8 0.8 copy.47
  93.6 0.2 copy-done.10
  93.8 0.0 copy-start.9
  93.8 0.7 copy.48
  94.5 0.3 copy-done.9
  94.8 0.0 copy-start.8
  94.8 0.7 copy.49
  95.4 0.3 copy-done.8
  95.7 0.0 copy-start.7
  95.7 0.7 copy.50
  96.4 0.3 copy-done.7
  96.7 0.0 copy-start.13
  96.7 0.0 copy-start.6
  96.7 0.7 copy.51
  97.3 0.0 copy-done.13
  97.4 0.5 copy.52
  97.9 0.0 copy-done.6
  97.9 0.0 copy-start.5
  97.9 0.7 copy.53
  98.5 0.3 copy-done.5
  98.8 0.0 copy-start.4
  98.8 0.7 copy.54
  99.5 0.3 copy-done.4
  99.8 0.0 copy-start.3
  99.8 0.7 copy.55
  100.4 0.3 copy-done.3
  100.7 0.0 copy-start.12
  100.7 0.7 copy.56
  101.4 0.0 copy-done.12
  101.4 0.5 copy.57
Async XLA Ops:
  87.1 0.7 copy-start.11
  88.4 1.9 %copy-start.2 = (bf16[1024,256]{1,0:T(8,128)(2,1)S(1)}, bf16[1024,256]{1,0:T(8,128)(2,1)}, u32[]{:S(2)}) copy-start(bf16[1024,256]{1,0:T(8,128)(2,1)} %get-tuple-element.61) | copy-start | bytes 1572868
  90.3 1.2 %copy-start.1 = (bf16[1024,256]{1,0:T(8,128)(2,1)S(1)}, bf16[1024,256]{1,0:T(8,128)(2,1)}, u32[]{:S(2)}) copy-start(bf16[1024,256]{1,0:T(8,128)(2,1)} %get-tuple-element.62) | copy-start | bytes 1572868
  91.6 1.2 %copy-start = (bf16[256,1024]{1,0:T(8,128)(2,1)S(1)}, bf16[256,1024]{1,0:T(8,128)(2,1)}, u32[]{:S(2)}) copy-start(bf16[256,1024]{1,0:T(8,128)(2,1)} %get-tuple-element.63) | copy-start | bytes 1572868
  92.8 1.0 %copy-start.10 = (f32[128,256]{1,0:T(8,128)S(1)}, f32[128,256]{1,0:T(8,128)}, u32[]{:S(2)}) copy-start(f32[128,256]{1,0:T(8,128)} %get-tuple-element.65) | copy-start | bytes 393220
  93.8 1.0 copy-start.9
  94.8 1.0 copy-start.8
  95.7 1.0 copy-start.7
  96.7 0.7 copy-start.13
  96.7 1.2 %copy-start.6 = (f32[128,256]{1,0:T(8,128)S(1)}, f32[128,256]{1,0:T(8,128)}, u32[]{:S(2)}) copy-start(f32[128,256]{1,0:T(8,128)} %get-tuple-element.70) | copy-start | bytes 393220
  97.9 1.0 copy-start.5
  98.8 1.0 copy-start.4
  99.8 1.0 copy-start.3
  100.7 0.7 copy-start.12

commit v2 on v1

--- a/solution.py
+++ b/solution.py
@@ -20,20 +20,22 @@
 
 
 def kernel(n, models, *refs):
-    slopes, slope_norm = refs[0:4], refs[4]
-    params, param_norm = refs[5:9], refs[9]
-    states, state_norm = refs[10:14], refs[14]
-    halves, half_norm = refs[15:19], refs[19]
-    nexts, next_norm = refs[20:24], refs[24]
-    state_news, state_new_norm = refs[25:29], refs[29]
+    slopes_far, slope_norm = refs[0:4], refs[4]
+    params_far, param_norm = refs[5:9], refs[9]
+    states_far, state_norm = refs[10:14], refs[14]
+    halves_far, half_norm = refs[15:19], refs[19]
+    nexts_far, next_norm = refs[20:24], refs[24]
+    state_news_far, state_new_norm = refs[25:29], refs[29]
     pair, ups, downs, totals = refs[30:34], refs[34:38], refs[38:42], refs[42:46]
+    slopes, params, states = refs[46:50], refs[50:54], refs[54:58]
+    halves, nexts, state_news = refs[58:62], refs[62:66], refs[66:70]
     (
         own_sizes, mean_sizes, vector, parts,
         pair_send, pair_recv, up_send, up_recv, down_send, down_recv,
         give_up_send, give_up_recv, give_down_send, give_down_recv, give_pair_send, give_pair_recv,
         own_send, own_recv, mean_send, mean_recv,
-        parts_send, parts_recv, norm_send, norm_recv,
-    ) = refs[46:]
+        parts_send, parts_recv, norm_send, norm_recv, near,
+    ) = refs[70:]
     outer = n // INNER
     rate = n ** (-0.5)
     me = lax.axis_index("replica")
@@ -52,7 +54,7 @@
         return ref.at[:, pl.ds(pl.multiple_of(b * columns, columns), columns)]
 
     def raw(m, b):
-        return block(m, slopes[m].at[0], b)
+        return block(m, slopes[m], b)
 
     def remote(src, dst, send_sem, recv_sem, device):
         return pltpu.make_async_remote_copy(
@@ -101,6 +103,24 @@
     def norm_copy(k):
         peer = lax.rem(me + k, n)
         return peer, remote(half_norm.at[me], half_norm.at[me], norm_send.at[k], norm_recv.at[me], {"replica": peer})
+
+    def load_slope(m):
+        return pltpu.make_async_copy(slopes_far[m].at[0], slopes[m], near.at[0, m])
+
+    def load_param(m):
+        return pltpu.make_async_copy(params_far[m], params[m], near.at[1, m])
+
+    def load_state(m):
+        return pltpu.make_async_copy(states_far[m], states[m], near.at[2, m])
+
+    def store_half(m):
+        return pltpu.make_async_copy(halves[m], halves_far[m], near.at[3, m])
+
+    def store_next(m):
+        return pltpu.make_async_copy(nexts[m], nexts_far[m], near.at[4, m])
+
+    def store_state(m):
+        return pltpu.make_async_copy(state_news[m], state_news_far[m], near.at[5, m])
 
     def local_sum(m, d):
         return raw(m, d * INNER + y)[...].astype(jnp.float32) + pair[m][d].astype(jnp.float32)
@@ -192,6 +212,8 @@
             give_down(m, z).start()
 
         give_pair(m, z, y).start()
+        store_next(m).start()
+        store_state(m).start()
 
     def relay(m):
         for k in range(1, outer):
@@ -220,6 +242,7 @@
     def close(m):
         for s in range(outer):
             give_pair(m, s, 1 - y).wait_recv()
+        store_half(m).start()
         for s in range(outer):
             pair_copy(m, s).wait_send()
             give_pair(m, s, y).wait_send()
@@ -257,46 +280,74 @@
         for k in range(1, n):
             norm_copy(k)[1].start()
 
+    for load in (load_slope, load_param, load_state):
+        for m in range(4):
+            load(m).start()
     barrier = pltpu.get_barrier_semaphore()
     for k in range(1, n):
         pl.semaphore_signal(barrier, inc=1, device_id={"replica": lax.rem(me + k, n)}, device_id_type=MESH)
     for k in range(1, models):
         pl.semaphore_signal(barrier, inc=1, device_id={"model": lax.rem(here + k, models)}, device_id_type=MESH)
-    for m in range(4):
-        own_sizes[here, m] = sizes(m, params[m][...])
     vector[...] = slope_norm[...].astype(jnp.float32)
     parts[me] = vector[:, pl.ds(pl.multiple_of(me * width, width), width)]
     pl.semaphore_wait(barrier, n - 1 + models - 1)
 
     for m in range(4):
+        load_slope(m).wait()
         for i in range(outer):
             pair_copy(m, turn(i)).start()
-        if m == 0:
-            for k in range(1, models):
-                own_copy(k)[1].start()
-            for k in range(1, n):
-                parts_copy(k)[1].start()
+    for k in range(1, n):
+        parts_copy(k)[1].start()
+    for m in range(4):
+        load_param(m).wait()
+        load_state(m).wait()
+        own_sizes[here, m] = sizes(m, params[m][...])
+    for k in range(1, models):
+        own_copy(k)[1].start()
 
     send_sums(0)
     vector_update()
     for k in range(1, models):
         peer = lax.rem(here + k, models)
         remote(own_sizes.at[peer], own_sizes.at[peer], own_send.at[k], own_recv.at[peer], {"model": peer}).wait_recv()
-    send_sums(1)
-    finish_sum(0)
-    send_sums(2)
-    update(0)
-    finish_sum(1)
-    send_sums(3)
-    update(1)
-    relay(0)
-    finish_sum(2)
-    update(2)
-    relay(1)
-    finish_sum(3)
-    relay(2)
-    update(3)
-    relay(3)
+    inside = jnp.logical_and(z > 0, z < outer - 1)
+
+    @pl.when(inside)
+    def _():
+        finish_sum(0)
+        send_sums(1)
+        update(0)
+        finish_sum(1)
+        send_sums(2)
+        update(1)
+        finish_sum(2)
+        relay(0)
+        send_sums(3)
+        update(2)
+        finish_sum(3)
+        relay(1)
+        update(3)
+        relay(2)
+        relay(3)
+
+    @pl.when(jnp.logical_not(inside))
+    def _():
+        send_sums(1)
+        finish_sum(0)
+        send_sums(2)
+        update(0)
+        finish_sum(1)
+        send_sums(3)
+        update(1)
+        finish_sum(2)
+        relay(0)
+        update(2)
+        finish_sum(3)
+        relay(1)
+        update(3)
+        relay(2)
+        relay(3)
+
     for m in range(4):
         close(m)
     for k in range(1, models):
@@ -306,6 +357,36 @@
         remote(half_norm.at[peer], half_norm.at[peer], norm_send.at[k], norm_recv.at[peer], {"replica": peer}).wait_recv()
         parts_copy(k)[1].wait_send()
         norm_copy(k)[1].wait_send()
+    for m in range(4):
+        store_next(m).wait()
+        store_state(m).wait()
+        store_half(m).wait()
+
+
+def place_kernel(count, *refs):
+    sources, targets, held = refs[0:count], refs[count : 2 * count], refs[2 * count : 3 * count]
+    come, go = refs[3 * count :]
+    into = [pltpu.make_async_copy(a, b, come.at[i]) for i, (a, b) in enumerate(zip(sources, held))]
+    out = [pltpu.make_async_copy(a, b, go.at[i]) for i, (a, b) in enumerate(zip(held, targets))]
+    for copy in into:
+        copy.start()
+    for i in range(count):
+        into[i].wait()
+        out[i].start()
+    for copy in out:
+        copy.wait()
+
+
+def placed(arrays):
+    count = len(arrays)
+    anywhere = [pl.BlockSpec(memory_space=pl.ANY)] * count
+    return pl.pallas_call(
+        functools.partial(place_kernel, count),
+        out_shape=[jax.ShapeDtypeStruct(a.shape, a.dtype) for a in arrays],
+        in_specs=anywhere,
+        out_specs=anywhere,
+        scratch_shapes=[pltpu.VMEM(a.shape, a.dtype) for a in arrays] + [pltpu.SemaphoreType.DMA((count,))] * 2,
+    )(*arrays)
 
 
 def fused(n, models, *args):
@@ -325,6 +406,10 @@
         [pltpu.VMEM((outer,) + s, jnp.bfloat16) for s in shapes]
         + [pltpu.VMEM((outer,) + s, jnp.float32) for s in shapes] * 2
         + [pltpu.VMEM(s, jnp.float32) for s in shapes]
+        + [pltpu.VMEM(s.shape[1:], jnp.bfloat16) for s in slopes[0:4]]
+        + [pltpu.VMEM(s, jnp.float32) for s in shapes] * 2
+        + [pltpu.VMEM(s.shape[1:], jnp.bfloat16) for s in slopes[0:4]]
+        + [pltpu.VMEM(s, jnp.float32) for s in shapes] * 2
         + [
             pltpu.VMEM((models, 4, 8, shapes[0][0]), jnp.float32),
             pltpu.VMEM((4, models, 8, shapes[0][0]), jnp.float32),
@@ -335,16 +420,21 @@
         + [dma(models)] * 2
         + [dma(4, models)] * 2
         + [dma(n)] * 4
+        + [dma(6, 4)]
     )
+    specs = ([pl.BlockSpec(memory_space=pl.ANY)] * 4 + [pl.BlockSpec(memory_space=pltpu.VMEM)]) * 3
     outs = pl.pallas_call(
         functools.partial(kernel, n, models),
         out_shape=out_shape,
-        in_specs=[pl.BlockSpec(memory_space=pltpu.VMEM)] * 15,
-        out_specs=[pl.BlockSpec(memory_space=pltpu.VMEM)] * 15,
+        in_specs=specs,
+        out_specs=specs,
         scratch_shapes=scratch,
         compiler_params=pltpu.CompilerParams(collective_id=0, has_side_effects=True),
     )(*slopes, *params[0:4], row(params[4]), *states[0:4], row(states[4]))
     outs = list(outs)
+    moved = [i for i in range(15) if i != 4]
+    for i, a in zip(moved, placed([outs[i] for i in moved])):
+        outs[i] = a
     outs[4] = outs[4].reshape(-1).astype(jnp.bfloat16)
     outs[9] = outs[9].reshape(-1)
     outs[14] = outs[14].reshape(-1)

time: 102 us -> 91.8 us (0.900)
  local copies, waits for them, and re-layouts: 14.1 us -> 0.67 us
  Pallas kernels: 86.5 us -> 89.6 us
    unnamed x42 -> x2, local copies, waits for them, and re-layouts: 14.1 us -> 0.67 us
    pallas_call x0 -> x1, Pallas kernels: none -> 2.95 us  [placed(): pl.pallas_call(functools.partial(place_kernel, count), out_shape=[jax.Sha...]
where the time goes in v2:
time: 91.8 us; the launch traced here: 91.6 us
  Pallas kernels  89.6 us (98%)
    pallas_call x1, Pallas kernels, fused(): pl.pallas_call(functools.partial(kernel, n, models), out_shape=out_shape,...  86.7 us
    pallas_call x1, Pallas kernels, placed(): pl.pallas_call(functools.partial(place_kernel, count), out_shape=[jax.Sha...  2.95 us

profile of v2, /device:TPU:0, one launch (start us, length us, event | category | flops | bytes accessed | tf_op | source)
XLA Modules:
  0.0 91.6 jit_solution(1570083161542349531)
XLA Ops:
  0.7 86.7 %shard_map.262 = (bf16[1024,256]{1,0:T(8,128)(2,1)}, bf16[1024,256]{1,0:T(8,128)(2,1)}, bf16[1024,256]{1,0:T(8,128)(2,1)}, bf16[256,1024]{1,0:T(8,128)(2,1)}, f3...) custom-call(bf16[1,1024,256]{2,1,0:T(8,128)(2,1)} %refs_0_.1, ...), custom_call_target="tpu_custom_call" | custom-call | tf_op jit(solution)/shard_map/pallas_call | solution.py:426
  87.3 3.0 %shard_map.263 = (bf16[1024,256]{1,0:T(8,128)(2,1)}, bf16[1024,256]{1,0:T(8,128)(2,1)}, bf16[1024,256]{1,0:T(8,128)(2,1)}, bf16[256,1024]{1,0:T(8,128)(2,1)}, f3...) custom-call(bf16[1024,256]{1,0:T(8,128)(2,1)} %get-tuple-element.44., ...), custom_call_target="tpu_custom_call" | custom-call | tf_op jit(solution)/shard_map/pallas_call | solution.py:383
  90.3 0.0 copy-start
  90.3 0.7 copy-done
  91.0 0.6 convert_reduce_fusion
Async XLA Ops:
  90.3 0.7 copy-start

commit v3 on v2

--- a/solution.py
+++ b/solution.py
@@ -321,12 +321,12 @@
         send_sums(2)
         update(1)
         finish_sum(2)
-        relay(0)
         send_sums(3)
         update(2)
+        relay(0)
         finish_sum(3)
+        update(3)
         relay(1)
-        update(3)
         relay(2)
         relay(3)
 
@@ -340,11 +340,11 @@
         send_sums(3)
         update(1)
         finish_sum(2)
+        update(2)
         relay(0)
-        update(2)
         finish_sum(3)
+        update(3)
         relay(1)
-        update(3)
         relay(2)
         relay(3)
 

time: 91.8 us -> 95.7 us (1.042)
  Pallas kernels: 89.6 us -> 93.5 us
    pallas_call x1, Pallas kernels: 86.7 us -> 90.6 us  [fused(): pl.pallas_call(functools.partial(kernel, n, models), out_shape=out_shape,...]
where the time goes in v3:
time: 95.7 us; the launch traced here: 95.5 us
  Pallas kernels  93.5 us (98%)
    pallas_call x1, Pallas kernels, fused(): pl.pallas_call(functools.partial(kernel, n, models), out_shape=out_shape,...  90.6 us
    pallas_call x1, Pallas kernels, placed(): pl.pallas_call(functools.partial(place_kernel, count), out_shape=[jax.Sha...  2.95 us

profile of v3, /device:TPU:0, one launch (start us, length us, event | category | flops | bytes accessed | tf_op | source)
XLA Modules:
  0.0 95.5 jit_solution(1454363158014189021)
XLA Ops:
  0.7 90.6 %shard_map.262 = (bf16[1024,256]{1,0:T(8,128)(2,1)}, bf16[1024,256]{1,0:T(8,128)(2,1)}, bf16[1024,256]{1,0:T(8,128)(2,1)}, bf16[256,1024]{1,0:T(8,128)(2,1)}, f3...) custom-call(bf16[1,1024,256]{2,1,0:T(8,128)(2,1)} %refs_0_.1, ...), custom_call_target="tpu_custom_call" | custom-call | tf_op jit(solution)/shard_map/pallas_call | solution.py:426
  91.2 3.0 %shard_map.263 = (bf16[1024,256]{1,0:T(8,128)(2,1)}, bf16[1024,256]{1,0:T(8,128)(2,1)}, bf16[1024,256]{1,0:T(8,128)(2,1)}, bf16[256,1024]{1,0:T(8,128)(2,1)}, f3...) custom-call(bf16[1024,256]{1,0:T(8,128)(2,1)} %get-tuple-element.44., ...), custom_call_target="tpu_custom_call" | custom-call | tf_op jit(solution)/shard_map/pallas_call | solution.py:383
  94.2 0.0 copy-start
  94.2 0.7 copy-done
  94.9 0.6 convert_reduce_fusion
Async XLA Ops:
  94.2 0.7 copy-start
